TPU v7x, 512 devices: a whole 4x4x16 slice. The times are simulated.
512 devices in a mesh: sample: 4 (over y), row: 8 (over x, core), col: 16 (over z).
Axes of the slice: x: 4, y: 4, z: 16, core: 2. Of those that a mesh axis runs over, the one named last changes fastest.
Arguments:
- pair: bfloat16 [3584, 896, 128], P(('sample', 'row'), 'col'), parts along dimension 0, may hold values from -6 to 6
- pair_gain: float32 [128], replicated, may hold values from 0.1 to 1.9
- bias_weight: bfloat16 [128, 16], replicated, may hold values from -0.5 to 0.5
- single: bfloat16 [3584, 384], P(('sample', 'row', 'col')), parts along dimension 0, may hold values from -50 to 50
- w_query: bfloat16 [384, 384], replicated, may hold values from -0.30618622 to 0.30618622
- w_key: bfloat16 [384, 384], replicated, may hold values from -0.30618622 to 0.30618622
- w_value: bfloat16 [384, 384], replicated, may hold values from -0.3125 to 0.3125
- w_out: bfloat16 [384, 384], replicated, may hold values from -0.3125 to 0.3125
- key_mask: int32 [3584], P(('sample', 'col')), parts along dimension 0, may hold values from 0 to 1, as said below
- out_grad: bfloat16 [3584, 384], P(('sample', 'row', 'col')), parts along dimension 0, may hold values from -6 to 6
Outputs:
- pair_grad: bfloat16 [3584, 896, 128], P(('sample', 'row'), 'col'), parts along dimension 0
- single_grad: bfloat16 [3584, 384], P(('sample', 'row', 'col')), parts along dimension 0
- query_weight_grad: float32 [1536, 384], P(('sample', 'row', 'col')), parts along dimension 0
- key_weight_grad: float32 [1536, 384], P(('sample', 'row', 'col')), parts along dimension 0
- value_weight_grad: float32 [1536, 384], P(('sample', 'row', 'col')), parts along dimension 0
- out_weight_grad: float32 [1536, 384], P(('sample', 'row', 'col')), parts along dimension 0
- bias_weight_grad: float32 [512, 16], P('sample'), parts along dimension 0
- gain_grad: float32 [512], P('sample'), parts along dimension 0
There are 4 independent parts, one for each index of `sample`. A program takes and returns all parts, laid end to end along the dimension named above; an argument that names none is the same for every part. Nothing has to cross between parts.
Inputs may be any that keep to these rules, and one draw needn't show every extreme that they name: key_mask is 1 exactly on a prefix of the tokens whose length is a multiple of 4, at least half of 896 and at most 892, and 0 after it.
All inputs are finite; a program needn't handle non-finite values.
Results may differ from a plain program's by a relative error of at most 0.04.
Values may be sent and summed in bfloat16 or wider, within the bound.
No kernel may reach another device: no remote copies, remote signals or barrier semaphores. Data moves between devices by JAX's collectives and lax.ppermute only.
A program may use at most 64 MiB of HBM per device.

v0:
```python
import functools

import jax
import jax.numpy as jnp
from jax import lax
from jax.sharding import Mesh
from jax.sharding import PartitionSpec as P

HEADS = 16
HEAD = 24
ROW = ("row_0", "row_1")
ROW_COL = ("row_0", "row_1", "col")
SAMPLE_ROW = ("sample", "row_0", "row_1")
SAMPLE_ROW_COL = ("sample", "row_0", "row_1", "col")


norm_eps = 1e-05
masked_score = -1000000000.0
highest = lax.Precision.HIGHEST


def laid_out(pieces, dim):
    shape = list(pieces.shape[1:])
    shape[dim] *= pieces.shape[0]
    return jnp.moveaxis(pieces, 0, dim).reshape(shape)


def stacked_from(array, axes, sequence):
    pieces = array[None]
    for k in sequence:
        pieces = lax.all_gather(pieces, axes[k], axis=0, tiled=True)
    carried = [lax.axis_size(axes[k]) for k in reversed(sequence)]
    pieces = pieces.reshape(*carried, *array.shape)
    turned = sorted(range(len(sequence)), key=lambda place: sequence[len(sequence) - 1 - place])
    return pieces.transpose(*turned, *range(len(sequence), pieces.ndim)).reshape(-1, *array.shape)


def gather_axes(array, axes, sequence, dim):
    return laid_out(stacked_from(array, axes, sequence), dim)


def from_everyone(array, axis):
    devices = lax.axis_size(axis)
    return lax.all_to_all(
        jnp.broadcast_to(array[None], (devices, *array.shape)), axis, 0, 0, tiled=True
    )


def gather_directly(array, axis, dim):
    pieces = from_everyone(array, axis)
    return laid_out(pieces, dim)


def collected_together(array, axis):
    leaves = jax.tree.leaves(array)
    sequence = sorted(range(len(leaves)), key=lambda k: -leaves[k].size)
    width = (1, *leaves[sequence[0]].shape)[-1]
    lines = [
        jnp.pad(leaves[k].reshape(-1), (0, -leaves[k].size % width)).reshape(-1, width)
        for k in sequence
    ]
    both, at, found = (from_everyone(jnp.concatenate(lines), axis), 0, {})
    for k, line in zip(sequence, lines):
        slab = both[:, at : at + len(line)].reshape(len(both), -1)
        found[k] = slab[:, : leaves[k].size].reshape(-1, *leaves[k].shape)
        at += len(line)
    numbers = iter(range(len(leaves)))
    return jax.tree.map(lambda _: found[next(numbers)], array)


def joined_by_halves(pieces, combine):
    while len(jax.tree.leaves(pieces)[0]) > 1:
        pieces = jax.vmap(combine)(
            *(jax.tree.map(lambda part: part[side::2], pieces) for side in (0, 1))
        )
    return jax.tree.map(lambda part: part[0], pieces)


def joined_all(array, axis, combine):
    pieces = collected_together(array, axis)
    return joined_by_halves(pieces, combine)


def over_pieces(array, axis):
    pieces = lax.all_gather(array, axis)
    return pieces.sum(axis=0)


def over_axes(array, axes):
    return functools.reduce(lax.psum, axes, array)


def taken_together(array, axis):
    everything = from_everyone(array, axis)
    return jnp.sum(everything.astype(jnp.float32), axis=0)


def broadcast(array, axis, root):
    return lax.dynamic_index_in_dim(lax.all_gather(array, axis), root, 0, keepdims=False)


def split_up(array, dim, devices):
    before, after = (array.shape[:dim], array.shape[dim + 1 :])
    return jnp.moveaxis(array.reshape(*before, devices, -1, *after), dim, 0)


def sum_at_owner(array, axis, dim):
    devices = lax.axis_size(axis)
    pieces = lax.all_to_all(split_up(array, dim, devices), axis, 0, 0, tiled=True)
    return jnp.sum(pieces.astype(jnp.float32), axis=0)


def sent_together(arrays, axis, dim, along):
    widths = [a.shape[along] for a in arrays]
    both = jnp.concatenate(arrays, axis=along)
    filled = sum_at_owner(both, axis, dim)
    return tuple(jnp.split(filled, [sum(widths[:k]) for k in range(1, len(widths))], axis=along))


def combine_stats(first, second):
    joint_top = jnp.maximum(first[0], second[0])
    joint_total = first[1] * jnp.exp(first[0] - joint_top) + second[1] * jnp.exp(
        second[0] - joint_top
    )
    return (joint_top, joint_total)


def project(grads, weight):
    return jnp.dot(grads, weight.astype(jnp.float32).T, precision=highest)


def transposed_product(left, right):
    return jnp.einsum("te,td->ed", left.astype(jnp.float32), right, precision=highest)


def body(pair, pair_gain, bias_weight, single, w_query, w_key, w_value, w_out, key_mask, out_grad):
    f32 = jnp.float32
    bf16 = jnp.bfloat16
    row_count = pair.shape[0]
    col_count = pair.shape[1]
    own_count = single.shape[0]
    model_width = single.shape[1]
    rows_total = lax.axis_size(ROW)
    cols_total = lax.axis_size("col")
    row_index = lax.axis_index(ROW)
    col_index = lax.axis_index("col")
    score_scale = HEAD ** (-0.5)
    all_single = gather_axes(single, ROW_COL, (2, 0, 1), 0)
    single_rows = lax.dynamic_slice_in_dim(all_single, row_index * row_count, row_count, 0)
    single_cols = lax.dynamic_slice_in_dim(all_single, col_index * col_count, col_count, 0)
    grad_rows = gather_directly(out_grad, "col", 0)
    query_rows = jnp.dot(single_rows, w_query, preferred_element_type=f32).astype(bf16)
    key_cols = jnp.dot(single_cols, w_key, preferred_element_type=f32).astype(bf16)
    value_cols = jnp.dot(single_cols, w_value, preferred_element_type=f32).astype(bf16)
    pair_float = pair.astype(f32)
    centred = pair_float - jnp.mean(pair_float, axis=2, keepdims=True)
    inverse = lax.rsqrt(jnp.mean(centred * centred, axis=2, keepdims=True) + norm_eps)
    normed = centred * inverse
    pair_normed = (normed * pair_gain).astype(bf16)
    pair_bias = jnp.einsum("ijc,ch->hij", pair_normed, bias_weight, preferred_element_type=f32)
    query_heads = query_rows.reshape(row_count, HEADS, HEAD)
    key_heads = key_cols.reshape(col_count, HEADS, HEAD)
    value_heads = value_cols.reshape(col_count, HEADS, HEAD)
    scores = (
        jnp.einsum("ihd,jhd->hij", query_heads, key_heads, preferred_element_type=f32) * score_scale
        + pair_bias
    )
    scores = jnp.where(key_mask[None, None, :] > 0, scores, masked_score)
    local_top = jnp.max(scores, axis=2)
    local_exp = jnp.exp(scores - local_top[:, :, None])
    row_top, row_total = joined_all((local_top, jnp.sum(local_exp, axis=2)), "col", combine_stats)
    exp_scores = local_exp * jnp.exp(local_top - row_top)[:, :, None]
    probs = exp_scores / row_total[:, :, None]
    probs_low = probs.astype(bf16)
    attended_part = jnp.einsum(
        "hij,jhd->ihd", probs_low, value_heads, preferred_element_type=f32
    ).reshape(row_count, model_width)
    attended = over_pieces(attended_part, "col")
    attended_low = attended.astype(bf16)
    grad_att = jnp.dot(grad_rows, w_out.T, preferred_element_type=f32).astype(bf16)
    grad_heads = grad_att.reshape(row_count, HEADS, HEAD)
    grad_probs = jnp.einsum("ihd,jhd->hij", grad_heads, value_heads, preferred_element_type=f32)
    row_delta = jnp.einsum(
        "ihd,ihd->hi", grad_heads.astype(f32), attended.reshape(row_count, HEADS, HEAD)
    )
    grad_scores = probs * (grad_probs - row_delta[:, :, None])
    grad_low = grad_scores.astype(bf16)
    query_grad = (
        jnp.einsum("hij,jhd->ihd", grad_low, key_heads, preferred_element_type=f32) * score_scale
    ).reshape(row_count, model_width)
    key_grad = (
        jnp.einsum("hij,ihd->jhd", grad_low, query_heads, preferred_element_type=f32) * score_scale
    ).reshape(col_count, model_width)
    value_grad = jnp.einsum(
        "hij,ihd->jhd", probs_low, grad_heads, preferred_element_type=f32
    ).reshape(col_count, model_width)
    grad_normed = jnp.einsum("hij,ch->ijc", grad_low, bias_weight, preferred_element_type=f32)
    bias_grad_part = jnp.einsum("ijc,hij->ch", pair_normed, grad_low, preferred_element_type=f32)
    gain_grad_part = jnp.sum(grad_normed * normed, axis=(0, 1))
    bias_weight_grad, gain_grad = (
        over_axes(bias_grad_part, ROW_COL),
        over_axes(gain_grad_part, ROW_COL),
    )
    scaled = grad_normed * pair_gain
    pair_grad = (
        inverse
        * (
            scaled
            - jnp.mean(scaled, axis=2, keepdims=True)
            - normed * jnp.mean(scaled * normed, axis=2, keepdims=True)
        )
    ).astype(bf16)
    own_start = col_index * own_count
    query_sum = taken_together(query_grad.astype(jnp.bfloat16), "col").astype(jnp.float32)
    key_sum, value_sum = (
        taken_together(key_grad.astype(jnp.bfloat16), ROW).astype(jnp.float32),
        taken_together(value_grad.astype(jnp.bfloat16), ROW).astype(jnp.float32),
    )
    own_query = lax.dynamic_slice_in_dim(query_sum, own_start, own_count, 0)
    own_part = project(own_query, w_query)
    key_side = project(key_sum, w_key) + project(value_sum, w_value)
    spread = cols_total // rows_total
    token_start = (row_index * cols_total + col_index) * own_count
    own_root = token_start // col_count
    offset = token_start - own_root * col_count
    for branch in range(spread):
        root_col = row_index * spread + branch
        fetched = broadcast(key_side.astype(jnp.bfloat16), "col", root_col).astype(key_side.dtype)
        piece = lax.dynamic_slice_in_dim(fetched, offset, own_count, 0)
        own_part = own_part + jnp.where(own_root == root_col, piece, 0.0)
    single_grad = own_part.astype(bf16)
    rows_each = model_width // (rows_total * cols_total)
    picked = lax.dynamic_index_in_dim(
        single_rows.reshape(row_count, rows_total, cols_total, rows_each),
        col_index,
        2,
        keepdims=False,
    ).reshape(row_count, rows_total * rows_each)
    att_picked = lax.dynamic_index_in_dim(
        attended_low.reshape(row_count, rows_total, cols_total, rows_each),
        col_index,
        2,
        keepdims=False,
    ).reshape(row_count, rows_total * rows_each)
    query_terms = transposed_product(picked, query_sum)
    out_terms = jnp.einsum("te,td->ed", att_picked, grad_rows, preferred_element_type=f32)
    query_weight_grad, out_weight_grad = sent_together(
        (query_terms.astype(jnp.bfloat16), out_terms.astype(jnp.bfloat16)), ROW, 0, 1
    )
    col_slab = lax.dynamic_slice_in_dim(
        single_cols, row_index * cols_total * rows_each, cols_total * rows_each, 1
    )
    key_weight_grad, value_weight_grad = sent_together(
        (
            transposed_product(col_slab, key_sum).astype(jnp.bfloat16),
            transposed_product(col_slab, value_sum).astype(jnp.bfloat16),
        ),
        "col",
        0,
        1,
    )
    return (
        pair_grad,
        single_grad,
        query_weight_grad,
        key_weight_grad,
        value_weight_grad,
        out_weight_grad,
        bias_weight_grad,
        gain_grad,
    )


def solution(mesh):
    split = Mesh(
        mesh.devices.reshape(mesh.shape["sample"], 4, 2, mesh.shape["col"]),
        ("sample", "row_0", "row_1", "col"),
    )
    placed = (
        P(SAMPLE_ROW, "col", None),
        P(),
        P(),
        P(SAMPLE_ROW_COL, None),
        P(),
        P(),
        P(),
        P(),
        P(("sample", "col")),
        P(SAMPLE_ROW_COL, None),
    )
    return jax.shard_map(
        body,
        mesh=split,
        in_specs=placed,
        out_specs=(
            P(SAMPLE_ROW, "col", None),
            P(SAMPLE_ROW_COL, None),
            P(SAMPLE_ROW_COL, None),
            P(SAMPLE_ROW_COL, None),
            P(SAMPLE_ROW_COL, None),
            P(SAMPLE_ROW_COL, None),
            P("sample", None),
            P("sample"),
        ),
        check_vma=False,
    )
```

profile of v0, /device:TPU:24, one launch (start us, length us, event | category | flops | bytes accessed | tf_op | source)
XLA Modules:
  0.0 360.0 jit_solution(5775855662982069744)
XLA Ops:
  10.3 3.0 fusion.12
  13.4 36.0 %all-gather.2 = bf16[16,7,384]{2,1,0:T(8,128)(2,1)S(1)} all-gather(bf16[1,7,384]{2,1,0:T(8,128)(2,1)S(1)} %bitcast.105), channel_id=2, replica_groups=mesh['sample'=4,'row_0'=4,'row_1'=2,'col'=16] {'col'}, dimensions={0}, use_global_device_ids=true | all-gather | bytes 91392 | tf_op jit(solution)/shard_map/all_gather | solution.py:31
  49.5 12.8 %all_gather.21 = bf16[64,7,384]{2,0,1:T(8,128)(2,1)S(1)} all-gather(bf16[16,7,384]{2,0,1:T(8,128)(2,1)S(1)} %copy.76), channel_id=1, replica_groups=mesh['sample'=4,'row_0'=4,'row_1'=2,'col'=16] {'row_0'}, dimensions={0}, use_global_device_ids=true | all-gather | bytes 430080 | tf_op jit(solution)/shard_map/all_gather | solution.py:31
  68.5 3.3 fusion.23
  74.6 6.7 %all-to-all-start = ((f32[16,32,112]{2,1,0:T(8,128)}), f32[16,32,112]{2,1,0:T(8,128)S(1)}, u32[]{:S(2)}, u32[]{:S(2)}) async-start(f32[16,32,112]{2,1,0:T(8,128)} %broadcast_in_dim.31), calls=%async_computation | async-start | bytes 524288 | tf_op jit(solution)/shard_map/all_to_all | solution.py:44
  82.5 17.3 %all-to-all-done = f32[16,32,112]{2,1,0:T(8,128)S(1)} async-done(((f32[16,32,112]{2,1,0:T(8,128)}), f32[16,32,112]{2,1,0:T(8,128)S(1)}, u32[]{:S(2)}, u32[]{:S(2)}) %all-to-all-start) | async-done | bytes 229408 | tf_op jit(solution)/shard_map/all_to_all | solution.py:44
  101.7 6.0 %all-to-all-start.1 = ((bf16[16,7,384]{2,1,0:T(8,128)(2,1)}), bf16[16,7,384]{2,1,0:T(8,128)(2,1)S(1)}, u32[]{:S(2)}, u32[]{:S(2)}) async-start(bf16[16,7,384]{2,1,0:T(8,128)(2,1)} %broadcast_in_dim.32), calls=%async_computation.1 | async-start | bytes 196608 | tf_op jit(solution)/shard_map/all_to_all | solution.py:44
  107.6 13.7 %all-to-all-done.1 = bf16[16,7,384]{2,1,0:T(8,128)(2,1)S(1)} async-done(((bf16[16,7,384]{2,1,0:T(8,128)(2,1)}), bf16[16,7,384]{2,1,0:T(8,128)(2,1)S(1)}, u32[]{:S(2)}, u32[]{:S(2)}) %all-to-all-start.1) | async-done | bytes 86048 | tf_op jit(solution)/shard_map/all_to_all | solution.py:44
  123.9 3.8 %all-to-all-start.4 = ((bf16[8,56,384]{2,1,0:T(8,128)(2,1)}), bf16[8,56,384]{2,1,0:T(8,128)(2,1)S(1)}, u32[]{:S(2)}, u32[]{:S(2)}) async-start(bf16[8,56,384]{2,1,0:T(8,128)(2,1)} %broadcast_in_dim.35), calls=%async_computation.4 | async-start | bytes 688128 | tf_op jit(solution)/shard_map/all_to_all | solution.py:44
  127.7 42.6 %all-gather.5.cloned.1.call-done = f32[16,112,384]{2,1,0:T(8,128)} async-done(((f32[1,112,384]{2,1,0:T(8,128)}), f32[16,112,384]{2,1,0:T(8,128)}) %all-gather.5.cloned.1.call-update) | async-done | bytes 2752528 | tf_op jit(solution)/shard_map/all_gather | solution.py:85
  174.8 4.1 %all-to-all-start.3 = ((bf16[8,56,384]{2,1,0:T(8,128)(2,1)}), bf16[8,56,384]{2,1,0:T(8,128)(2,1)S(1)}, u32[]{:S(2)}, u32[]{:S(2)}) async-start(bf16[8,56,384]{2,1,0:T(8,128)(2,1)} %broadcast_in_dim.34), calls=%async_computation.3 | async-start | bytes 688128 | tf_op jit(solution)/shard_map/all_to_all | solution.py:44
  180.0 7.2 %all-to-all-done.3 = bf16[8,56,384]{2,1,0:T(8,128)(2,1)S(1)} async-done(((bf16[8,56,384]{2,1,0:T(8,128)(2,1)}), bf16[8,56,384]{2,1,0:T(8,128)(2,1)S(1)}, u32[]{:S(2)}, u32[]{:S(2)}) %all-to-all-start.3) | async-done | bytes 344096 | tf_op jit(solution)/shard_map/all_to_all | solution.py:44
  189.1 7.5 %all-to-all-start.6 = ((bf16[16,3,768]{2,1,0:T(4,128)(2,1)}), bf16[16,3,768]{2,1,0:T(4,128)(2,1)S(1)}, u32[]{:S(2)}, u32[]{:S(2)}) async-start(bf16[16,3,768]{2,1,0:T(4,128)(2,1)} %reshape.139), calls=%async_computation.6 | async-start | bytes 196608 | tf_op jit(solution)/shard_map/all_to_all | solution.py:109
  197.8 12.2 %all-to-all-done.6 = bf16[16,3,768]{2,1,0:T(4,128)(2,1)S(1)} async-done(((bf16[16,3,768]{2,1,0:T(4,128)(2,1)}), bf16[16,3,768]{2,1,0:T(4,128)(2,1)S(1)}, u32[]{:S(2)}, u32[]{:S(2)}) %all-to-all-start.6) | async-done | bytes 73760 | tf_op jit(solution)/shard_map/all_to_all | solution.py:109
  211.3 3.7 %all-to-all-start.2 = ((bf16[16,112,384]{2,1,0:T(8,128)(2,1)}), bf16[16,112,384]{2,1,0:T(8,128)(2,1)S(1)}, u32[]{:S(2)}, u32[]{:S(2)}) async-start(bf16[16,112,384]{2,1,0:T(8,128)(2,1)} %broadcast_in_dim.33), calls=%async_computation.2 | async-start | bytes 2752512 | tf_op jit(solution)/shard_map/all_to_all | solution.py:44
  225.4 3.8 %convolution_bitcast_fusion = f32[128,16]{0,1:T(8,128)S(1)} fusion(bf16[16,112,56]{2,0,1:T(8,128)(2,1)} %copy.85, bf16[112,56,128]{2,1,0:T(8,128)(2,1)S(1)} %copy-done.1, f32[128]{0:T(128)S(1)} %copy-done.28, f32[112,56]{1,0:T(8,128)} %copy-done.22, f32[112,56]{1,0:T(8,128)} %copy-done.17), kind=kOutput, calls=%fused_computation.41 | convolution fusion | flops 29704192 | bytes 1865216 | tf_op jit(solution)/shard_map/ijc,hij->ch/dot_general | solution.py:198
  229.2 6.4 %fusion.11 = (f32[128]{0:T(128)S(1)}, f32[112,56]{1,0:T(8,128)S(1)}, f32[112,56]{1,0:T(8,128)}, f32[112,56,128]{2,1,0:T(8,128)}) fusion(bf16[112,56,128]{2,1,0:T(8,128)(2,1)S(1)} %copy-done.1, f32[112,56]{1,0:T(8,128)S(1)} %copy-done.23, f32[112,56]{1,0:T(8,128)S(1)} %copy-done.18, f32[128]{0:T(128)} %param.11, bf16[16,112,56]{2,0,1:T(8,128)(2,1)S(1)} %copy-done.19, ...), kind=kOutput, calls=%fused_computation.13 | convolution fusion | flops 32902784 | bytes 5123072 | tf_op jit(solution)/shard_map/hij,ch->ijc/dot_general | solution.py:197
  235.7 9.6 %all-reduce.1 = (f32[128,16]{0,1:T(8,128)S(1)}, f32[128]{0:T(128)}) all-reduce(f32[128,16]{0,1:T(8,128)S(1)} %convolution_bitcast_fusion, f32[128]{0:T(128)S(1)} %get-tuple-element.8), channel_id=1, replica_groups=mesh['sample'=4,'row_0'=4,'row_1'=2,'col'=16] {'row_0'}, use_global_device_ids=true, to_apply=%region_12.13 | all-reduce | flops 2176 | bytes 17408 | tf_op jit(solution)/shard_map/psum | solution.py:90
  245.2 2.6 all-reduce.2
  247.8 52.7 %all-reduce = (f32[128,16]{0,1:T(8,128)}, f32[128]{0:T(128)}) all-reduce(f32[128,16]{0,1:T(8,128)S(1)} %get-tuple-element.15, f32[128]{0:T(128)S(1)} %get-tuple-element.16), channel_id=1, replica_groups=mesh['sample'=4,'row_0'=4,'row_1'=2,'col'=16] {'col'}, use_global_device_ids=true, to_apply=%region_14.15 | all-reduce | flops 2176 | bytes 17408 | tf_op jit(solution)/shard_map/psum | solution.py:90
  302.3 7.7 %fusion.10 = bf16[112,56,128]{2,1,0:T(8,128)(2,1)} fusion(bf16[112,56,128]{2,1,0:T(8,128)(2,1)S(1)} %copy-done.1, f32[112,56,128]{2,1,0:T(8,128)} %get-tuple-element.31, f32[112,56]{1,0:T(8,128)S(1)} %get-tuple-element.32, f32[112,56]{1,0:T(8,128)S(1)} %get-tuple-element.33, f32[128]{0:T(128)} %param.11, f32[112,56]{1,0:T(8,128)S(1)} %copy-done.23, ...), kind=kLoop, calls=%fused_computation.12 | loop fusion | flops 7225344 | bytes 6523392 | tf_op jit(solution)/shard_map/convert_element_type | solution.py:212
  310.8 31.2 %all-gather.1 = bf16[896,384]{1,0:T(8,128)(2,1)S(1)} all-gather(bf16[56,384]{1,0:T(8,128)(2,1)S(1)} %fusion.19), channel_id=3, replica_groups=mesh['sample'=4,'row_0'=4,'row_1'=2,'col'=16] {'col'}, dimensions={0}, use_global_device_ids=true | all-gather | bytes 731136 | tf_op jit(solution)/shard_map/all_gather | solution.py:99
  343.7 3.3 all-to-all-start.5
  348.1 4.5 %all-to-all-done.5 = bf16[8,3,768]{2,1,0:T(4,128)(2,1)S(1)} async-done(((bf16[8,3,768]{2,1,0:T(4,128)(2,1)}), bf16[8,3,768]{2,1,0:T(4,128)(2,1)S(1)}, u32[]{:S(2)}, u32[]{:S(2)}) %all-to-all-start.5) | async-done | bytes 36896 | tf_op jit(solution)/shard_map/all_to_all | solution.py:109
  (138 shorter events, 43.4 us)
Async XLA Ops:
  7.2 60.9 %copy-start = (bf16[384,384]{1,0:T(8,128)(2,1)S(1)}, bf16[384,384]{1,0:T(8,128)(2,1)}, u32[]{:S(2)}) copy-start(bf16[384,384]{1,0:T(8,128)(2,1)} %param.14) | copy-start | bytes 884740
  10.2 58.2 %copy-start.17 = (f32[112,56]{1,0:T(8,128)}, f32[112,56]{1,0:T(8,128)S(1)}, u32[]{:S(2)}) copy-start(f32[112,56]{1,0:T(8,128)S(1)} %broadcast_multiply_fusion.2) | copy-start | bytes 75268
  10.3 55.8 %copy-start.3 = (bf16[384,384]{1,0:T(8,128)(2,1)S(1)}, bf16[384,384]{1,0:T(8,128)(2,1)}, u32[]{:S(2)}) copy-start(bf16[384,384]{1,0:T(8,128)(2,1)} %param.15) | copy-start | bytes 884740
  13.3 55.1 %copy-start.1 = (bf16[112,56,128]{2,1,0:T(8,128)(2,1)S(1)}, bf16[112,56,128]{2,1,0:T(8,128)(2,1)}, u32[]{:S(2)}) copy-start(bf16[112,56,128]{2,1,0:T(8,128)(2,1)} %param.10) | copy-start | bytes 4816900
  13.3 55.1 %copy-start.28 = (f32[128]{0:T(128)S(1)}, f32[128]{0:T(128)}, u32[]{:S(2)}) copy-start(f32[128]{0:T(128)} %param.11) | copy-start | bytes 1540
  13.3 55.1 %copy-start.29 = (bf16[128,16]{0,1:T(8,128)(2,1)S(1)}, bf16[128,16]{0,1:T(8,128)(2,1)}, u32[]{:S(2)}) copy-start(bf16[128,16]{0,1:T(8,128)(2,1)} %param.12) | copy-start | bytes 12292
  13.4 58.4 %copy-start.22 = (f32[112,56]{1,0:T(8,128)}, f32[112,56]{1,0:T(8,128)S(1)}, u32[]{:S(2)}) copy-start(f32[112,56]{1,0:T(8,128)S(1)} %add_rsqrt_fusion) | copy-start | bytes 75268
  73.3 27.7 %copy-start.27 = (bf16[7,384]{1,0:T(8,128)(2,1)S(1)}, bf16[7,384]{1,0:T(8,128)(2,1)}, u32[]{:S(2)}) copy-start(bf16[7,384]{1,0:T(8,128)(2,1)} %param.19) | copy-start | bytes 16132
  74.6 25.2 %all-to-all-start = ((f32[16,32,112]{2,1,0:T(8,128)}), f32[16,32,112]{2,1,0:T(8,128)S(1)}, u32[]{:S(2)}, u32[]{:S(2)}) async-start(f32[16,32,112]{2,1,0:T(8,128)} %broadcast_in_dim.31), calls=%async_computation | async-start | bytes 524288 | tf_op jit(solution)/shard_map/all_to_all | solution.py:44
  81.3 89.0 %all-gather.5.cloned.1.call-start = ((), (), s32[]{:S(2)}) async-start(), calls=%async_computation.7 | async-start | bytes 2924544 | tf_op jit(solution)/shard_map/all_gather | solution.py:85
  82.4 40.6 %copy-start.24 = (bf16[56,384]{0,1:T(8,128)(2,1)}, bf16[56,384]{0,1:T(8,128)(2,1)S(1)}, u32[]{:S(2)}) copy-start(bf16[56,384]{0,1:T(8,128)(2,1)S(1)} %copy.82) | copy-start | bytes 129028
  101.7 19.7 %all-to-all-start.1 = ((bf16[16,7,384]{2,1,0:T(8,128)(2,1)}), bf16[16,7,384]{2,1,0:T(8,128)(2,1)S(1)}, u32[]{:S(2)}, u32[]{:S(2)}) async-start(bf16[16,7,384]{2,1,0:T(8,128)(2,1)} %broadcast_in_dim.32), calls=%async_computation.1 | async-start | bytes 196608 | tf_op jit(solution)/shard_map/all_to_all | solution.py:44
  123.9 49.7 %copy-start.9 = (bf16[112,384]{0,1:T(8,128)(2,1)S(1)}, bf16[112,384]{0,1:T(8,128)(2,1)}, u32[]{:S(2)}) copy-start(bf16[112,384]{0,1:T(8,128)(2,1)} %copy-done.8) | copy-start | bytes 258052
  123.9 50.1 %all-to-all-start.4 = ((bf16[8,56,384]{2,1,0:T(8,128)(2,1)}), bf16[8,56,384]{2,1,0:T(8,128)(2,1)S(1)}, u32[]{:S(2)}, u32[]{:S(2)}) async-start(bf16[8,56,384]{2,1,0:T(8,128)(2,1)} %broadcast_in_dim.35), calls=%async_computation.4 | async-start | bytes 688128 | tf_op jit(solution)/shard_map/all_to_all | solution.py:44
  172.2 25.5 %copy-start.2 = (f32[112,384]{1,0:T(8,128)}, f32[112,384]{1,0:T(8,128)S(1)}, u32[]{:S(2)}) copy-start(f32[112,384]{1,0:T(8,128)S(1)} %reduce_sum.111) | copy-start | bytes 516100
  174.8 12.5 %all-to-all-start.3 = ((bf16[8,56,384]{2,1,0:T(8,128)(2,1)}), bf16[8,56,384]{2,1,0:T(8,128)(2,1)S(1)}, u32[]{:S(2)}, u32[]{:S(2)}) async-start(bf16[8,56,384]{2,1,0:T(8,128)(2,1)} %broadcast_in_dim.34), calls=%async_computation.3 | async-start | bytes 688128 | tf_op jit(solution)/shard_map/all_to_all | solution.py:44
  178.9 32.3 %copy-start.15 = (f32[56,384]{1,0:T(8,128)}, f32[56,384]{1,0:T(8,128)S(1)}, u32[]{:S(2)}) copy-start(f32[56,384]{1,0:T(8,128)S(1)} %convert_reduce_fusion.2) | copy-start | bytes 258052
  187.3 24.0 %copy-start.13 = (f32[56,384]{1,0:T(8,128)}, f32[56,384]{1,0:T(8,128)S(1)}, u32[]{:S(2)}) copy-start(f32[56,384]{1,0:T(8,128)S(1)} %convert_reduce_fusion.3) | copy-start | bytes 258052
  189.1 20.9 %all-to-all-start.6 = ((bf16[16,3,768]{2,1,0:T(4,128)(2,1)}), bf16[16,3,768]{2,1,0:T(4,128)(2,1)S(1)}, u32[]{:S(2)}, u32[]{:S(2)}) async-start(bf16[16,3,768]{2,1,0:T(4,128)(2,1)} %reshape.139), calls=%async_computation.6 | async-start | bytes 196608 | tf_op jit(solution)/shard_map/all_to_all | solution.py:109
  211.3 131.4 %all-to-all-start.2 = ((bf16[16,112,384]{2,1,0:T(8,128)(2,1)}), bf16[16,112,384]{2,1,0:T(8,128)(2,1)S(1)}, u32[]{:S(2)}, u32[]{:S(2)}) async-start(bf16[16,112,384]{2,1,0:T(8,128)(2,1)} %broadcast_in_dim.33), calls=%async_computation.2 | async-start | bytes 2752512 | tf_op jit(solution)/shard_map/all_to_all | solution.py:44
  229.2 71.3 %copy-start.12 = (bf16[112,384]{1,0:T(8,128)(2,1)S(1)}, bf16[112,384]{1,0:T(8,128)(2,1)}, u32[]{:S(2)}) copy-start(bf16[112,384]{1,0:T(8,128)(2,1)} %copy-done.11) | copy-start | bytes 258052
  302.3 39.8 %copy-start.21 = (bf16[16,3,768]{2,1,0:T(4,128)(2,1)S(1)}, bf16[16,3,768]{2,1,0:T(4,128)(2,1)}, u32[]{:S(2)}) copy-start(bf16[16,3,768]{2,1,0:T(4,128)(2,1)} %copy-done.20) | copy-start | bytes 221188
  309.9 32.9 %copy-start.25 = (bf16[112,24]{0,1:T(8,128)(2,1)S(1)}, bf16[112,24]{0,1:T(8,128)(2,1)}, u32[]{:S(2)}) copy-start(bf16[112,24]{0,1:T(8,128)(2,1)} %reshape.136) | copy-start | bytes 16132
  343.7 8.8 %all-to-all-start.5 = ((bf16[8,3,768]{2,1,0:T(4,128)(2,1)}), bf16[8,3,768]{2,1,0:T(4,128)(2,1)S(1)}, u32[]{:S(2)}, u32[]{:S(2)}) async-start(bf16[8,3,768]{2,1,0:T(4,128)(2,1)} %reshape.138), calls=%async_computation.5 | async-start | bytes 98304 | tf_op jit(solution)/shard_map/all_to_all | solution.py:109
  (14 other events, 91.4 us)
Sparse Core Ops, SparseCore 0:
  101.1 69.1 all-gather.4
where the time goes:
time: 363 us; the launch traced here: 360 us
  blocking collectives  147 us (40%)
  waiting for transfers between devices  97.5 us (27%)
  starting transfers between devices  35.2 us (10%)
  matrix products  25.4 us (7%)
  local copies, waits for them, and re-layouts  21.3 us (6%)
  other arithmetic  18.7 us (5%)
  between operations  14.8 us (4%)
    psum x3, blocking collectives, over_axes(): return functools.reduce(lax.psum, axes, array)  64.9 us
    all_gather x3, blocking collectives, stacked_from(): pieces = lax.all_gather(pieces, axes[k], axis=0, tiled=True)  51.1 us
    all_gather x1, waiting for transfers between devices, over_pieces(): pieces = lax.all_gather(array, axis)  42.6 us
    all_to_all x5, waiting for transfers between devices, from_everyone(): lax.all_to_all(jnp.broadcast_to(array[None], (devices, *array.shape)), ax...  38.3 us
    all_gather x1, blocking collectives, broadcast(): lax.all_gather(array, axis)  31.2 us
    all_to_all x5, starting transfers between devices, from_everyone(): lax.all_to_all(jnp.broadcast_to(array[None], (devices, *array.shape)), ax...  24.3 us
    all_to_all x2, waiting for transfers between devices, sum_at_owner(): lax.all_to_all(split_up(array, dim, devices), axis, 0, 0, tiled=True)  16.7 us
    all_to_all x2, starting transfers between devices, sum_at_owner(): lax.all_to_all(split_up(array, dim, devices), axis, 0, 0, tiled=True)  10.8 us
  transfers between devices with their start and end apart: 8, of which 6 were waited for; matrix products, arithmetic and copies ran while one was open for 12% of the time, Pallas kernels for 0%

commit v1 on v0

v1 whole, which is shorter than its diff:
```python
import functools

import jax
import jax.numpy as jnp
from jax import lax
from jax.experimental import pallas as pl
from jax.experimental.pallas import tpu as pltpu
from jax.sharding import Mesh
from jax.sharding import PartitionSpec as P

HEADS = 16
HEAD = 24
ROW = ("row_0", "row_1")
SAMPLE_ROW = ("sample", "row_0", "row_1")
SAMPLE_ROW_COL = ("sample", "row_0", "row_1", "col")

norm_eps = 1e-05
masked_score = -1000000000.0
score_scale = HEAD ** (-0.5)
f32 = jnp.float32
bf16 = jnp.bfloat16

OWN = 7
CHUNKS = 16
SLOTS = 128
LANES = SLOTS * HEADS
KEYS = 56
ROWS = 8
EDGE = 48
WIDTH = 384
PAIR = 128


def nn(a, b):
    return lax.dot_general(a, b, (((1,), (0,)), ((), ())), preferred_element_type=f32)


def nt(a, b):
    return lax.dot_general(a, b, (((1,), (1,)), ((), ())), preferred_element_type=f32)


def tn(a, b):
    return lax.dot_general(a, b, (((0,), (0,)), ((), ())), preferred_element_type=f32)


def expander():
    slot = lax.broadcasted_iota(jnp.int32, (SLOTS, 1), 0)
    lane = lax.broadcasted_iota(jnp.int32, (1, LANES), 1) // HEADS
    return jnp.where(slot == lane, 1.0, 0.0).astype(bf16)


def own_head():
    feature = (lax.broadcasted_iota(jnp.int32, (WIDTH, 1), 0) * 2731) >> 16
    head = lax.broadcasted_iota(jnp.int32, (1, LANES), 1) % HEADS
    return feature == head


def normalized(x):
    centred = x - jnp.mean(x, axis=-1, keepdims=True)
    inverse = lax.rsqrt(jnp.mean(centred * centred, axis=-1, keepdims=True) + norm_eps)
    return centred * inverse, inverse


def bias_kernel(pair_ref, gain_ref, spread_ref, normed_ref, bias_ref):
    gain = gain_ref[...]
    parts = []
    for t in range(OWN):
        normed, _ = normalized(pair_ref[t].astype(f32))
        parts.append((normed * gain).astype(bf16))
    block = jnp.concatenate(parts, axis=1)
    normed_ref[0] = block
    bias_ref[...] = nn(block, spread_ref[...])


def query_kernel(gathered_ref, w_query_ref, w_out_ref, query_ref, grad_ref, rows_t_ref, grads_ref):
    everything = gathered_ref[...].astype(f32)
    rows = everything[:, 0:8, :].reshape(SLOTS, WIDTH)
    grads = everything[:, 8:16, :].reshape(SLOTS, WIDTH).astype(bf16)
    rows_t_ref[...] = rows.T.astype(bf16)
    grads_ref[...] = grads
    spread = expander()
    mask = own_head()
    query = nn(rows.astype(bf16), w_query_ref[...])
    grad_att = nt(grads, w_out_ref[...])
    query_ref[...] = jnp.where(mask, nn(query.T.astype(bf16), spread), 0.0).astype(bf16)
    grad_ref[...] = jnp.where(mask, nn(grad_att.T.astype(bf16), spread), 0.0).astype(bf16)


def score_kernel(
    source_ref, cols_ref, w_key_ref, w_value_ref, mask_ref, bias_ref, query_ref, grad_ref,
    exp_ref, grad_probs_ref, stats_ref, key_t_ref, value_t_ref, cols_t_ref,
):
    padded = cols_ref[source_ref[0]]
    token = lax.broadcasted_iota(jnp.int32, (KEYS, 8 * ROWS), 0)
    slot = lax.broadcasted_iota(jnp.int32, (KEYS, 8 * ROWS), 1)
    pick = jnp.where((slot // 8) * OWN + slot % 8 == token, 1.0, 0.0)
    pick = jnp.where(slot % 8 < OWN, pick, 0.0).astype(bf16)
    cols = nn(pick, padded)
    cols_t_ref[...] = cols.T.astype(bf16)
    cols = cols.astype(bf16)
    key = nn(cols, w_key_ref[...])
    value = nn(cols, w_value_ref[...])
    key_t_ref[...] = key.T.astype(bf16)
    value_t_ref[...] = value.T.astype(bf16)
    scores = nn(key.astype(bf16), query_ref[...]) * score_scale + bias_ref[...]
    scores = jnp.where(mask_ref[...] > 0, scores, masked_score)
    top = jnp.max(scores, axis=0, keepdims=True)
    exp_scores = jnp.exp(scores - top)
    grad_probs = nn(value.astype(bf16), grad_ref[...])
    exp_ref[...] = exp_scores
    grad_probs_ref[...] = grad_probs
    total = jnp.sum(exp_scores, axis=0, keepdims=True)
    product = jnp.sum(exp_scores * grad_probs, axis=0, keepdims=True)
    tiles = [
        line[:, g * 128 : (g + 1) * 128] for line in (top, total, product) for g in range(CHUNKS)
    ]
    block = jnp.concatenate(tiles, axis=0)
    for k in range(CHUNKS):
        stats_ref[k] = block


def gradient_kernel(
    all_stats_ref, stats_ref, exp_ref, grad_probs_ref, query_ref, grad_ref, key_t_ref, value_t_ref,
    cols_t_ref, rows_t_ref, grads_ref, normed_ref, w_query_ref, w_key_ref, w_value_ref, source_ref,
    low_ref, own_ref, out_ref,
):
    tops = all_stats_ref[:, 0:CHUNKS, :]
    top = jnp.max(tops, axis=0)
    weight = jnp.exp(tops - top[None])
    total = jnp.sum(all_stats_ref[:, CHUNKS : 2 * CHUNKS, :] * weight, axis=0)
    product = jnp.sum(all_stats_ref[:, 2 * CHUNKS : 3 * CHUNKS, :] * weight, axis=0)
    factor = jnp.exp(stats_ref[0, 0:CHUNKS, :] - top) / total
    delta = product / total
    probs_parts, low_parts = [], []
    for g in range(CHUNKS):
        lanes = slice(g * 128, (g + 1) * 128)
        probs = exp_ref[:, lanes] * factor[g : g + 1, :]
        low = (probs * (grad_probs_ref[:, lanes] - delta[g : g + 1, :])).astype(bf16)
        probs_parts.append(probs.astype(bf16))
        low_parts.append(low)
    probs_low = jnp.concatenate(probs_parts, axis=1)
    grad_low = jnp.concatenate(low_parts, axis=1)
    low_ref[...] = grad_low
    mask = own_head()
    spread = expander()
    key_grad = (nt(grad_low, query_ref[...]) * score_scale).astype(bf16)
    value_grad = nt(probs_low, grad_ref[...]).astype(bf16)
    query_terms = jnp.where(mask, nn(key_t_ref[...], grad_low), 0.0).astype(bf16)
    query_grad = (nt(query_terms, spread) * score_scale).T.astype(bf16)
    attended_terms = jnp.where(mask, nn(value_t_ref[...], probs_low), 0.0).astype(bf16)
    attended_t = nt(attended_terms, spread).astype(bf16)
    own_ref[...] = nt(query_grad, w_query_ref[...])
    side = nt(key_grad, w_key_ref[...]) + nt(value_grad, w_value_ref[...])
    slot = lax.broadcasted_iota(jnp.int32, (8 * ROWS, KEYS), 0)
    token = lax.broadcasted_iota(jnp.int32, (8 * ROWS, KEYS), 1)
    place = jnp.where((slot // 8) * OWN + slot % 8 == token, 1.0, 0.0)
    place = jnp.where(slot % 8 < OWN, place, 0.0).astype(bf16)
    side = nn(place, side.astype(bf16)).astype(bf16)
    products = (
        nn(rows_t_ref[...], query_grad),
        nn(cols_t_ref[...], key_grad),
        nn(cols_t_ref[...], value_grad),
        nn(attended_t, grads_ref[...]),
    )
    for w, product_of in enumerate(products):
        product_of = product_of.astype(bf16)
        for r in range(ROWS):
            out_ref[r, w * EDGE : (w + 1) * EDGE, :] = product_of[r * EDGE : (r + 1) * EDGE, :]
    stacked = jnp.concatenate(low_parts, axis=0)
    wide = tn(stacked, normed_ref[...].reshape(CHUNKS * KEYS, OWN * PAIR))
    bias_grad = wide[0:HEADS, 0:PAIR]
    for t in range(1, OWN):
        bias_grad = bias_grad + wide[t * HEADS : (t + 1) * HEADS, t * PAIR : (t + 1) * PAIR]
    tail = jnp.concatenate(
        [bias_grad[0:8], bias_grad[8:16], jnp.zeros((8, WIDTH - 2 * PAIR), f32)], axis=1
    ).astype(bf16)
    empty = jnp.zeros((8 * ROWS, WIDTH), bf16)
    for r in range(ROWS):
        out_ref[r, 4 * EDGE : 4 * EDGE + 8 * ROWS, :] = jnp.where(source_ref[0] == r, side, empty)
        out_ref[r, 4 * EDGE + 8 * ROWS :, :] = tail


def middle_kernel(half_ref, arrived_ref, own_ref, out_ref):
    filled = arrived_ref[0].astype(f32)
    for r in range(1, ROWS):
        filled = filled + arrived_ref[r].astype(f32)
    weights = filled[0 : 4 * EDGE].astype(bf16)
    row = lax.broadcasted_iota(jnp.int32, (CHUNKS * 16, 4 * EDGE), 0)
    col = lax.broadcasted_iota(jnp.int32, (CHUNKS * 16, 4 * EDGE), 1)
    inner = row % 16
    kind = inner // 3
    wanted = kind * EDGE + (row // 16) * 3 + inner % 3
    turn = jnp.where(col == wanted, 1.0, 0.0)
    turn = jnp.where(inner < 12, turn, 0.0).astype(bf16)
    spread = nn(turn, weights).astype(bf16)
    side = filled[4 * EDGE : 4 * EDGE + 8 * ROWS]
    tail = filled[4 * EDGE + 8 * ROWS :]
    for k in range(CHUNKS):
        piece = own_ref[8 * k : 8 * k + 8, :]
        low = (k % 8) * 8
        piece = piece + jnp.where(half_ref[0] == k // 8, side[low : low + 8], 0.0)
        out_ref[k, 0:16, :] = jnp.concatenate([piece, tail], axis=0).astype(bf16)
        out_ref[k, 16:32, :] = spread[16 * k : 16 * k + 16]


def last_kernel(
    arrived_ref, gain_ref, bias_weight_t_ref, single_ref, query_ref, key_ref, value_ref, out_ref,
    bias_ref, gain_grad_ref,
):
    filled = arrived_ref[0].astype(f32)
    for k in range(1, CHUNKS):
        filled = filled + arrived_ref[k].astype(f32)
    single_ref[...] = filled[0:OWN].astype(bf16)
    query_ref[...] = filled[16:19]
    key_ref[...] = filled[19:22]
    value_ref[...] = filled[22:25]
    out_ref[...] = filled[25:28]
    bias_grad = jnp.concatenate([filled[8:16, 0:PAIR], filled[8:16, PAIR : 2 * PAIR]], axis=0)
    bias_ref[...] = bias_grad.T
    gain_grad_ref[...] = (
        jnp.sum(bias_grad * bias_weight_t_ref[...].astype(f32), axis=0, keepdims=True) / gain_ref[...]
    )


def pair_kernel(pair_ref, gain_ref, spread_ref, low_ref, out_ref):
    gain = gain_ref[...]
    wide = nn(low_ref[...], spread_ref[...])
    for t in range(OWN):
        normed, inverse = normalized(pair_ref[t].astype(f32))
        scaled = wide[:, t * PAIR : (t + 1) * PAIR] * gain
        first = jnp.mean(scaled, axis=-1, keepdims=True)
        second = jnp.mean(scaled * normed, axis=-1, keepdims=True)
        out_ref[t] = (inverse * (scaled - first - normed * second)).astype(bf16)


def whole():
    return pl.BlockSpec(memory_space=pltpu.VMEM)


def scalar():
    return pl.BlockSpec(memory_space=pltpu.SMEM)


def call(kernel, outs, *args, scalars=(), flops=1 << 20):
    return pl.pallas_call(
        kernel,
        out_shape=[jax.ShapeDtypeStruct(shape, kind) for shape, kind in outs],
        in_specs=[scalar() if k in scalars else whole() for k in range(len(args))],
        out_specs=[whole() for _ in outs],
        cost_estimate=pl.CostEstimate(flops=flops, bytes_accessed=1 << 20, transcendentals=0),
    )(*args)


def to_all(array, axes, devices):
    return lax.all_to_all(
        jnp.broadcast_to(array[None], (devices, *array.shape)), axes, 0, 0, tiled=True
    )


def body(pair, pair_gain, bias_weight, single, w_query, w_key, w_value, w_out, key_mask, out_grad):
    row_index = lax.axis_index(ROW)
    col_index = lax.axis_index("col")
    source = (col_index // 2).astype(jnp.int32)
    gain = pair_gain.reshape(1, PAIR)
    held = jnp.concatenate(
        [jnp.pad(single, ((0, 1), (0, 0))), jnp.pad(out_grad, ((0, 1), (0, 0)))], axis=0
    )
    gathered = to_all(held, "col", CHUNKS)

    eye = jnp.eye(OWN, 8, dtype=bf16)
    spread = (eye[:, None, :, None] * bias_weight[None, :, None, :]).reshape(OWN * PAIR, 128)
    normed, bias = pl.pallas_call(
        bias_kernel,
        grid=(CHUNKS,),
        in_specs=[
            pl.BlockSpec((OWN, KEYS, PAIR), lambda g: (g, 0, 0)),
            pl.BlockSpec((1, PAIR), lambda g: (0, 0)),
            pl.BlockSpec((OWN * PAIR, 128), lambda g: (0, 0)),
        ],
        out_specs=[
            pl.BlockSpec((1, KEYS, OWN * PAIR), lambda g: (g, 0, 0)),
            pl.BlockSpec((KEYS, 128), lambda g: (0, g)),
        ],
        out_shape=[
            jax.ShapeDtypeStruct((CHUNKS, KEYS, OWN * PAIR), bf16),
            jax.ShapeDtypeStruct((KEYS, LANES), f32),
        ],
        cost_estimate=pl.CostEstimate(
            flops=1 << 28, bytes_accessed=1 << 22, transcendentals=0
        ),
    )(pair, gain, spread)

    half = lax.dynamic_slice_in_dim(gathered, 8 * (col_index % 2), 8, 0)[:, 0:8]
    columns = to_all(half.reshape(8 * ROWS, WIDTH), ROW, ROWS)
    query, grad, rows_t, grads = call(
        query_kernel,
        [
            ((WIDTH, LANES), bf16),
            ((WIDTH, LANES), bf16),
            ((WIDTH, SLOTS), bf16),
            ((SLOTS, WIDTH), bf16),
        ],
        gathered, w_query, w_out,
        flops=1 << 28,
    )
    exp_scores, grad_probs, stats, key_t, value_t, cols_t = call(
        score_kernel,
        [
            ((KEYS, LANES), f32),
            ((KEYS, LANES), f32),
            ((CHUNKS, 3 * CHUNKS, 128), f32),
            ((WIDTH, KEYS), bf16),
            ((WIDTH, KEYS), bf16),
            ((WIDTH, KEYS), bf16),
        ],
        source.reshape(1), columns, w_key, w_value, key_mask.reshape(KEYS, 1), bias, query, grad,
        scalars=(0,),
    )
    all_stats = lax.all_to_all(stats, "col", 0, 0, tiled=True)
    grad_low, own_side, leaving = call(
        gradient_kernel,
        [
            ((KEYS, LANES), bf16),
            ((SLOTS, WIDTH), f32),
            ((ROWS, 4 * EDGE + 8 * ROWS + 8, WIDTH), bf16),
        ],
        all_stats, stats, exp_scores, grad_probs, query, grad, key_t, value_t, cols_t, rows_t, grads,
        normed, w_query, w_key, w_value, source.reshape(1),
        scalars=(15,),
    )
    arrived = lax.all_to_all(leaving, ROW, 0, 0, tiled=True)
    pair_grad = pl.pallas_call(
        pair_kernel,
        grid=(CHUNKS,),
        in_specs=[
            pl.BlockSpec((OWN, KEYS, PAIR), lambda g: (g, 0, 0)),
            pl.BlockSpec((1, PAIR), lambda g: (0, 0)),
            pl.BlockSpec((128, OWN * PAIR), lambda g: (0, 0)),
            pl.BlockSpec((KEYS, 128), lambda g: (0, g)),
        ],
        out_specs=pl.BlockSpec((OWN, KEYS, PAIR), lambda g: (g, 0, 0)),
        out_shape=jax.ShapeDtypeStruct(pair.shape, bf16),
        cost_estimate=pl.CostEstimate(
            flops=1 << 28, bytes_accessed=1 << 22, transcendentals=0
        ),
    )(pair, gain, spread.T, grad_low)
    half_here = jnp.where(row_index == source, col_index % 2, -1).astype(jnp.int32).reshape(1)
    (going,) = call(
        middle_kernel, [((CHUNKS, 32, WIDTH), bf16)], half_here, arrived, own_side, scalars=(0,)
    )
    landed = lax.all_to_all(going, "col", 0, 0, tiled=True)
    edge = ((3, WIDTH), f32)
    single_grad, query_grad, key_grad, value_grad, out_weight_grad, bias_grad, gain_grad = call(
        last_kernel,
        [((OWN, WIDTH), bf16), edge, edge, edge, edge, ((PAIR, HEADS), f32), ((1, PAIR), f32)],
        landed, gain, bias_weight.T,
    )
    return (
        pair_grad,
        single_grad,
        query_grad,
        key_grad,
        value_grad,
        out_weight_grad,
        bias_grad,
        gain_grad.reshape(PAIR),
    )


def solution(mesh):
    split = Mesh(
        mesh.devices.reshape(mesh.shape["sample"], 4, 2, mesh.shape["col"]),
        ("sample", "row_0", "row_1", "col"),
    )
    placed = (
        P(SAMPLE_ROW, "col", None),
        P(),
        P(),
        P(SAMPLE_ROW_COL, None),
        P(),
        P(),
        P(),
        P(),
        P(("sample", "col")),
        P(SAMPLE_ROW_COL, None),
    )
    return jax.shard_map(
        body,
        mesh=split,
        in_specs=placed,
        out_specs=(
            P(SAMPLE_ROW, "col", None),
            P(SAMPLE_ROW_COL, None),
            P(SAMPLE_ROW_COL, None),
            P(SAMPLE_ROW_COL, None),
            P(SAMPLE_ROW_COL, None),
            P(SAMPLE_ROW_COL, None),
            P("sample", None),
            P("sample"),
        ),
        check_vma=False,
    )
```

time: 363 us -> 162 us (0.45)
  blocking collectives: 147 us -> 30.4 us
  waiting for transfers between devices: 97.5 us -> 47.9 us
  Pallas kernels: 0 us -> 43.4 us
  matrix products: 25.4 us -> 0 us
  other arithmetic: 18.7 us -> 0.81 us
  between operations: 14.8 us -> 0.72 us
  local copies, waits for them, and re-layouts: 21.3 us -> 8.63 us
  starting transfers between devices: 35.2 us -> 29 us
    all_gather x4 -> x0, blocking collectives: 82.3 us -> none  [the longest x3 51.1 us: stacked_from(): pieces = lax.all_gather(pieces, axes[k], axis=0, tiled=True)]
    psum x3 -> x0, blocking collectives: 64.9 us -> none  [over_axes(): return functools.reduce(lax.psum, axes, array)]
    pallas_call x0 -> x7, Pallas kernels: none -> 43.4 us  [the longest x5 20.4 us: call(): pl.pallas_call(kernel, out_shape=[jax.ShapeDtypeStruct(shape, kind) for s...]
    all_gather x1 -> x0, waiting for transfers between devices: 42.6 us -> none  [over_pieces(): pieces = lax.all_gather(array, axis)]
    all_to_all x0 -> x1, blocking collectives: none -> 30.4 us  [body(): all_stats = lax.all_to_all(stats, 'col', 0, 0, tiled=True)]
    dot_general x20 -> x0, matrix products: 25.4 us -> none  [the longest x1 6.43 us: body(): jnp.einsum('hij,ch->ijc', grad_low, bias_weight, preferred_element_type=f32)]
    convert_element_type x2 -> x1, other arithmetic: 9.23 us -> 0.01 us  [body(): eye = jnp.eye(OWN, 8, dtype=bf16)]
    reduce_sum x9 -> x0, other arithmetic: 7.74 us -> none  [the longest x1 3.04 us: body(): jnp.mean(centred * centred, axis=2, keepdims=True) + norm_eps]
  transfers between devices with their start and end apart: 8 -> 4, of which waited for: 6 -> 3; matrix products, arithmetic and copies ran while one was open for 12% -> 2% of each run, Pallas kernels for 0% -> 17%
where the time goes in v1:
time: 162 us; the launch traced here: 161 us
  waiting for transfers between devices  47.9 us (30%)
  Pallas kernels  43.4 us (27%)
  blocking collectives  30.4 us (19%)
  starting transfers between devices  29 us (18%)
  local copies, waits for them, and re-layouts  8.63 us (5%)
    all_to_all x1, blocking collectives, body(): all_stats = lax.all_to_all(stats, 'col', 0, 0, tiled=True)  30.4 us
    all_to_all x1, waiting for transfers between devices, body(): arrived = lax.all_to_all(leaving, ROW, 0, 0, tiled=True)  22.1 us
    pallas_call x5, Pallas kernels, call(): pl.pallas_call(kernel, out_shape=[jax.ShapeDtypeStruct(shape, kind) for s...  20.4 us
    all_to_all x2, starting transfers between devices, to_all(): lax.all_to_all(jnp.broadcast_to(array[None], (devices, *array.shape)), ax...  19.5 us
    all_to_all x2, waiting for transfers between devices, to_all(): lax.all_to_all(jnp.broadcast_to(array[None], (devices, *array.shape)), ax...  15 us
    pallas_call x1, Pallas kernels, body(): pl.pallas_call(pair_kernel, grid=(CHUNKS,), in_specs=[pl.BlockSpec((OWN,...  11.6 us
    pallas_call x1, Pallas kernels, body(): pl.pallas_call(bias_kernel, grid=(CHUNKS,), in_specs=[pl.BlockSpec((OWN,...  11.4 us
    all_to_all x1, waiting for transfers between devices, body(): landed = lax.all_to_all(going, 'col', 0, 0, tiled=True)  10.8 us
  transfers between devices with their start and end apart: 4, of which 3 were waited for; matrix products, arithmetic and copies ran while one was open for 2% of the time, Pallas kernels for 17%

profile of v1, /device:TPU:24, one launch (start us, length us, event | category | flops | bytes accessed | tf_op | source)
XLA Modules:
  0.0 160.9 jit_solution(2349352523788536788)
XLA Ops:
  0.6 0.7 fusion.2
  2.1 15.2 %all-to-all-start = ((bf16[16,16,384]{2,1,0:T(8,128)(2,1)}), bf16[16,16,384]{2,1,0:T(8,128)(2,1)S(1)}, u32[]{:S(2)}, u32[]{:S(2)}) async-start(bf16[16,16,384]{2,1,0:T(8,128)(2,1)} %broadcast_in_dim.6), calls=%async_computation | async-start | bytes 393216 | tf_op jit(solution)/shard_map/all_to_all | solution.py:255
  17.3 1.3 copy.22.mask_ref
  18.6 15.0 %all-to-all-done.gathered_ref = bf16[16,16,384]{2,1,0:T(8,128)(2,1)S(1)} async-done(((bf16[16,16,384]{2,1,0:T(8,128)(2,1)}), bf16[16,16,384]{2,1,0:T(8,128)(2,1)S(1)}, u32[]{:S(2)}, u32[]{:S(2)}) %all-to-all-start) | async-done | bytes 196640 | tf_op jit(solution)/shard_map/all_to_all | solution.py:255
  33.7 0.8 broadcast_in_dim.8
  34.5 4.3 %all-to-all-start.1 = ((bf16[8,64,384]{2,1,0:T(8,128)(2,1)}), bf16[8,64,384]{2,1,0:T(8,128)(2,1)S(1)}, u32[]{:S(2)}, u32[]{:S(2)}) async-start(bf16[8,64,384]{2,1,0:T(8,128)(2,1)} %broadcast_in_dim.8), calls=%async_computation.1 | async-start | bytes 786432 | tf_op jit(solution)/shard_map/all_to_all | solution.py:255
  38.9 0.8 copy.21.spread_ref
  39.7 11.4 %shard_map.161 = (bf16[16,56,896]{2,1,0:T(8,128)(2,1)}, f32[56,2048]{1,0:T(8,128)}) custom-call(bf16[112,56,128]{2,1,0:T(8,128)(2,1)} %pair_ref.3, f32[1,128]{1,0:T(1,128)} %bitcast.26, bf16[896,128]{1,0:T(8,128)(2,1)} %copy.21.spread_ref), custom_call_target="tpu_custom_call" | custom-call | flops 268435456 | bytes 4194304 | tf_op jit(solution)/shard_map/pallas_call | solution.py:272
  51.1 3.7 %shard_map.162 = (bf16[384,2048]{1,0:T(8,128)(2,1)}, bf16[384,2048]{1,0:T(8,128)(2,1)}, bf16[384,128]{1,0:T(8,128)(2,1)}, bf16[128,384]{1,0:T(8,128)(2,1)}) custom-call(bf16[16,16,384]{2,1,0:T(8,128)(2,1)} %copy-done.3, bf16[384,384]{1,0:T(8,128)(2,1)} %w_query_ref.3, bf16[384,384]{1,0:T(8,128)(2,1)} %w_out_ref.1), custom_call_target="tpu_custom_call" | custom-call | flops 268435456 | bytes 1048576 | tf_op jit(solution)/shard_map/pallas_call | solution.py:245
  54.8 0.7 copy-done.2
  55.5 4.3 %shard_map.163 = (f32[56,2048]{1,0:T(8,128)}, f32[56,2048]{1,0:T(8,128)}, f32[16,48,128]{2,1,0:T(8,128)}, bf16[384,56]{1,0:T(8,128)(2,1)}, bf16[384,56]{1,0:T(8,128)(2,1)}, /*index=5*/bf16[384,56]{1,0:T(8,128)(2,1)}) custom-call(s32[1]{0:T(128)} %bitcast.2.source_ref, bf16[8,64,384]{2,1,0:T(8,128)(2,1)} %copy-done.2, bf16[384,384]{1,0:T(8,128)(2,1)} %w_key_ref.3, ...), custom_call_target="tpu_custom_call" | custom-call | flops 1048576 | bytes 1048576 | tf_op jit(solution)/shard_map/pallas_call | solution.py:245
  59.8 30.4 %all_to_all.25.all_stats_ref = f32[16,48,128]{2,1,0:T(8,128)} all-to-all(f32[16,48,128]{2,1,0:T(8,128)} %get-tuple-element.33.stats_ref), channel_id=1, replica_groups=mesh['sample'=4,'row_0'=4,'row_1'=2,'col'=16] {'col'}, dimensions={0} | all-to-all | bytes 786432 | tf_op jit(solution)/shard_map/all_to_all | solution.py:319
  90.3 8.1 %shard_map.164 = (bf16[56,2048]{1,0:T(8,128)(2,1)}, f32[128,384]{1,0:T(8,128)}, bf16[8,264,384]{2,1,0:T(8,128)(2,1)}) custom-call(f32[16,48,128]{2,1,0:T(8,128)} %all_to_all.25.all_stats_ref, f32[16,48,128]{2,1,0:T(8,128)} %get-tuple-element.33.stats_ref, f32[56,2048]{1,0:T(8,128)} %get-tuple-element.34.exp_ref, ...), custom_call_target="tpu_custom_call" | custom-call | flops 1048576 | bytes 1048576 | tf_op jit(solution)/shard_map/pallas_call | solution.py:245
  98.4 3.7 %all-to-all-start.3 = ((bf16[8,264,384]{2,1,0:T(8,128)(2,1)}), bf16[8,264,384]{2,1,0:T(8,128)(2,1)S(1)}, u32[]{:S(2)}, u32[]{:S(2)}) async-start(bf16[8,264,384]{2,1,0:T(8,128)(2,1)} %get-tuple-element.43), calls=%async_computation.3 | async-start | bytes 3244032 | tf_op jit(solution)/shard_map/all_to_all | solution.py:331
  102.0 22.1 %all-to-all-done.3.arrived_ref = bf16[8,264,384]{2,1,0:T(8,128)(2,1)S(1)} async-done(((bf16[8,264,384]{2,1,0:T(8,128)(2,1)}), bf16[8,264,384]{2,1,0:T(8,128)(2,1)S(1)}, u32[]{:S(2)}, u32[]{:S(2)}) %all-to-all-start.3) | async-done | bytes 1622048 | tf_op jit(solution)/shard_map/all_to_all | solution.py:331
  124.1 1.2 copy-done
  125.3 2.6 %shard_map.166 = bf16[16,32,384]{2,1,0:T(8,128)(2,1)} custom-call(s32[1]{0:T(128)} %bitcast.5.half_ref, bf16[8,264,384]{2,1,0:T(8,128)(2,1)} %copy-done, f32[128,384]{1,0:T(8,128)} %get-tuple-element.44.own_ref), custom_call_target="tpu_custom_call" | custom-call | flops 1048576 | bytes 1048576 | tf_op jit(solution)/shard_map/pallas_call | solution.py:245
  127.9 5.8 %all-to-all-start.4 = ((bf16[16,32,384]{2,1,0:T(8,128)(2,1)}), bf16[16,32,384]{2,1,0:T(8,128)(2,1)S(1)}, u32[]{:S(2)}, u32[]{:S(2)}) async-start(bf16[16,32,384]{2,1,0:T(8,128)(2,1)} %shard_map.166), calls=%async_computation.4 | async-start | bytes 786432 | tf_op jit(solution)/shard_map/all_to_all | solution.py:351
  133.7 0.7 copy.29
  134.4 11.6 %shard_map.165 = bf16[112,56,128]{2,1,0:T(8,128)(2,1)} custom-call(bf16[112,56,128]{2,1,0:T(8,128)(2,1)} %pair_ref.3, f32[1,128]{1,0:T(1,128)} %bitcast.27, bf16[128,896]{1,0:T(8,128)(2,1)} %bitcast.24, bf16[56,2048]{1,0:T(8,128)(2,1)} %get-tuple-element.42.low_ref), custom_call_target="tpu_custom_call" | custom-call | flops 268435456 | bytes 4194304 | tf_op jit(solution)/shard_map/pallas_call | solution.py:332
  146.0 10.8 %all-to-all-done.4.arrived_ref = bf16[16,32,384]{2,1,0:T(8,128)(2,1)S(1)} async-done(((bf16[16,32,384]{2,1,0:T(8,128)(2,1)}), bf16[16,32,384]{2,1,0:T(8,128)(2,1)S(1)}, u32[]{:S(2)}, u32[]{:S(2)}) %all-to-all-start.4) | async-done | bytes 393248 | tf_op jit(solution)/shard_map/all_to_all | solution.py:351
  156.9 0.8 copy-done.1
  157.6 1.8 %shard_map.167 = (bf16[7,384]{1,0:T(8,128)(2,1)}, f32[3,384]{1,0:T(4,128)}, f32[3,384]{1,0:T(4,128)}, f32[3,384]{1,0:T(4,128)}, f32[3,384]{1,0:T(4,128)}, /*index=5*/f32[128,16]{1,0:T(8,128)}, f32[1,128]{1,0:T(1,128)}) custom-call(bf16[16,32,384]{2,1,0:T(8,128)(2,1)} %copy-done.1, f32[1,128]{1,0:T(1,128)} %bitcast.28, bf16[16,128]{1,0:T(8,128)(2,1)} %bitcast.25), custom_call_target="tpu_custom_call" | custom-call | flops 1048576 | bytes 1048576 | tf_op jit(solution)/shard_map/pallas_call | solution.py:245
  159.4 1.5 copy.23
  (13 shorter events, 0.8 us)
Async XLA Ops:
  0.6 38.1 %copy-start.4 = (bf16[128,16]{0,1:T(8,128)(2,1)S(1)}, bf16[128,16]{0,1:T(8,128)(2,1)}, u32[]{:S(2)}) copy-start(bf16[128,16]{0,1:T(8,128)(2,1)} %param.12) | copy-start | bytes 12292
  2.1 31.6 %all-to-all-start = ((bf16[16,16,384]{2,1,0:T(8,128)(2,1)}), bf16[16,16,384]{2,1,0:T(8,128)(2,1)S(1)}, u32[]{:S(2)}, u32[]{:S(2)}) async-start(bf16[16,16,384]{2,1,0:T(8,128)(2,1)} %broadcast_in_dim.6), calls=%async_computation | async-start | bytes 393216 | tf_op jit(solution)/shard_map/all_to_all | solution.py:255
  33.6 17.5 %copy-start.3 = (bf16[16,16,384]{2,1,0:T(8,128)(2,1)}, bf16[16,16,384]{2,1,0:T(8,128)(2,1)S(1)}, u32[]{:S(2)}) copy-start(bf16[16,16,384]{2,1,0:T(8,128)(2,1)S(1)} %all-to-all-done.gathered_ref) | copy-start | bytes 589828
  34.5 20.3 %all-to-all-start.1 = ((bf16[8,64,384]{2,1,0:T(8,128)(2,1)}), bf16[8,64,384]{2,1,0:T(8,128)(2,1)S(1)}, u32[]{:S(2)}, u32[]{:S(2)}) async-start(bf16[8,64,384]{2,1,0:T(8,128)(2,1)} %broadcast_in_dim.8), calls=%async_computation.1 | async-start | bytes 786432 | tf_op jit(solution)/shard_map/all_to_all | solution.py:255
  54.8 0.7 copy-start.2
  98.4 25.7 %all-to-all-start.3 = ((bf16[8,264,384]{2,1,0:T(8,128)(2,1)}), bf16[8,264,384]{2,1,0:T(8,128)(2,1)S(1)}, u32[]{:S(2)}, u32[]{:S(2)}) async-start(bf16[8,264,384]{2,1,0:T(8,128)(2,1)} %get-tuple-element.43), calls=%async_computation.3 | async-start | bytes 3244032 | tf_op jit(solution)/shard_map/all_to_all | solution.py:331
  124.1 1.2 copy-start
  127.9 28.9 %all-to-all-start.4 = ((bf16[16,32,384]{2,1,0:T(8,128)(2,1)}), bf16[16,32,384]{2,1,0:T(8,128)(2,1)S(1)}, u32[]{:S(2)}, u32[]{:S(2)}) async-start(bf16[16,32,384]{2,1,0:T(8,128)(2,1)} %shard_map.166), calls=%async_computation.4 | async-start | bytes 786432 | tf_op jit(solution)/shard_map/all_to_all | solution.py:351
  156.9 0.8 copy-start.1
